TPU v7x, 32 devices: a whole 2x2x4 slice. The times are simulated.
32 devices in a mesh: pp: 4 (over x, core), tp: 4 (over z), dp: 2 (over y).
Axes of the slice: x: 2, y: 2, z: 4, core: 2. Of those that a mesh axis runs over, the one named last changes fastest.
Arguments:
- act_in: bfloat16 [4, 2, 128, 4096], P('pp', 'dp', 'tp'), may hold values from -6 to 6
- stash_in: bfloat16 [4, 2, 128, 4096], P('pp', 'dp', 'tp'), may hold values from -6 to 6
- grad_in: bfloat16 [4, 2, 128, 4096], P('pp', 'dp', 'tp'), may hold values from -6 to 6
- doc_ids: int32 [4, 2, 2, 128], P('pp', 'dp'), may hold values from 0 to 15, never falling along the last dimension, each value on 1 to 64 neighbouring positions
- query_weight: bfloat16 [4, 4096, 4096], P('pp', None, 'tp'), as said below
- key_weight: bfloat16 [4, 4096, 1024], P('pp', None, 'tp'), as said below
- value_weight: bfloat16 [4, 4096, 1024], P('pp', None, 'tp'), as said below
- out_weight: bfloat16 [4, 4096, 4096], P('pp', None, 'tp'), may hold values from -0.09375 to 0.09375
Outputs:
- act_out: bfloat16 [4, 2, 128, 4096], P('pp', 'dp', 'tp')
- grad_out: bfloat16 [4, 2, 128, 4096], P('pp', 'dp', 'tp')
- grad_query: float32 [4, 4096, 4096], P('pp', 'dp', 'tp')
- grad_key: float32 [4, 4096, 1024], P('pp', 'dp', 'tp')
- grad_value: float32 [4, 4096, 1024], P('pp', 'dp', 'tp')
Inputs may be any that keep to these rules, and one draw needn't show every extreme that they name: `doc_ids`: along each row of 128 positions the document numbers never fall. `query_weight`: entries of mean zero. `key_weight`: for each of the 8 key heads, its 1 stored copies (consecutive blocks of 128 columns) are equal; entries of mean zero. `value_weight`: for each of the 8 value heads, its 1 stored copies (consecutive blocks of 128 columns) are equal.
All inputs are finite; a program needn't handle non-finite values.
Results may differ from a plain program's by a relative error of at most 0.033.
Values may be sent and summed in bfloat16 or wider, within the bound.
A program may use at most 128 MiB of HBM per device.

v0:
```python
import math
import jax
import jax.numpy as jnp
from jax import lax
from jax.sharding import PartitionSpec as P

HEAD = 128
epsilon = 1e-05


def from_behind(value, axis, steps):
    count = lax.axis_size(axis)
    pairs = [(source, (source + steps) % count) for source in range(count)]
    return lax.ppermute(value, axis, pairs)


def norm_rows(token_rows):
    widened = token_rows.astype(jnp.float32)
    inverse = lax.rsqrt(jnp.mean(widened * widened, axis=-1, keepdims=True) + epsilon)
    return ((widened * inverse).astype(jnp.bfloat16), inverse)


def allowed(documents):
    length = documents.shape[0]
    position = jnp.arange(length, dtype=jnp.int32)
    return (position[None, :] <= position[:, None]) & (documents[:, None] == documents[None, :])


def project(normed, weight):
    return jnp.dot(normed, weight, preferred_element_type=jnp.float32).astype(jnp.bfloat16)


def contract_last(left_side, right_side):
    return lax.dot_general(
        left_side, right_side, (((1,), (1,)), ((), ())), preferred_element_type=jnp.float32
    )


def split_heads(queries, keys, values, kv_local):
    length = queries.shape[0]
    group_size = queries.shape[1] // (kv_local * HEAD)
    return (
        queries.reshape(length, kv_local, group_size, HEAD),
        keys.reshape(length, kv_local, HEAD),
        values.reshape(length, kv_local, HEAD),
    )


def attend_probs(query_heads, key_heads, allowed_pairs):
    scores = jnp.einsum(
        "ihgd,jhd->hgij", query_heads, key_heads, preferred_element_type=jnp.float32
    ) * (1.0 / math.sqrt(HEAD))
    scores = jnp.where(allowed_pairs, scores, -jnp.inf)
    row_max = jnp.max(scores, axis=-1, keepdims=True)
    weights = jnp.exp(scores - row_max)
    return (weights / jnp.sum(weights, axis=-1, keepdims=True)).astype(jnp.bfloat16)


def attend_back(dmixed, queries, keys, values, probs, kv_local):
    length = queries.shape[0]
    query_heads, key_heads, value_heads = split_heads(queries, keys, values, kv_local)
    dmixed_heads = dmixed.reshape(query_heads.shape)
    dprobs = jnp.einsum(
        "ihgd,jhd->hgij", dmixed_heads, value_heads, preferred_element_type=jnp.float32
    )
    weights = probs.astype(jnp.float32)
    inner = jnp.sum(weights * dprobs, axis=-1, keepdims=True)
    dscores = (weights * (dprobs - inner) * (1.0 / math.sqrt(HEAD))).astype(jnp.bfloat16)
    dqueries = jnp.einsum("hgij,jhd->ihgd", dscores, key_heads, preferred_element_type=jnp.float32)
    dkeys = jnp.einsum("hgij,ihgd->jhd", dscores, query_heads, preferred_element_type=jnp.float32)
    dvalues = jnp.einsum("hgij,ihgd->jhd", probs, dmixed_heads, preferred_element_type=jnp.float32)
    return (
        dqueries.astype(jnp.bfloat16).reshape(length, queries.shape[1]),
        dkeys.reshape(length, kv_local * HEAD),
        dvalues.reshape(length, kv_local * HEAD),
    )


def handoff(payload, offset):
    return from_behind(payload, "pp", offset)


def per_copy(left_side, right_side, copies):
    length = left_side.shape[0] // copies
    product = jnp.einsum(
        "nsd,nse->nde",
        left_side.reshape(copies, length, left_side.shape[1]),
        right_side.reshape(copies, length, right_side.shape[1]),
        preferred_element_type=jnp.float32,
    )
    kept = lax.optimization_barrier(product.astype(jnp.bfloat16))
    return jnp.sum(kept.astype(jnp.float32), axis=0)


def body(act_in, stash_in, grad_in, doc_ids, query_weight, key_weight, value_weight, out_weight):
    kv_local = key_weight.shape[2] // HEAD
    forward_rows = act_in[0, 0]
    backward_rows = stash_in[0, 0]
    grad_rows = grad_in[0, 0]
    normed_ahead, unused_inverse = norm_rows(forward_rows)
    normed_back, inverse_back = norm_rows(backward_rows)
    ahead_full, back_full, grad_full = (
        lax.all_gather(normed_ahead, "tp", axis=0, tiled=True),
        lax.all_gather(normed_back, "tp", axis=0, tiled=True),
        lax.all_gather(grad_rows, "tp", axis=0, tiled=True),
    )
    w_query = query_weight[0]
    w_key = key_weight[0]
    w_value = value_weight[0]
    w_out = out_weight[0]
    queries_ahead = project(ahead_full, w_query)
    keys_ahead = project(ahead_full, w_key)
    values_ahead = project(ahead_full, w_value)
    query_heads, key_heads, value_heads = split_heads(
        queries_ahead, keys_ahead, values_ahead, kv_local
    )
    probs_ahead = attend_probs(query_heads, key_heads, allowed(doc_ids[0, 0, 0]))
    mixed_ahead = jnp.einsum(
        "hgij,jhd->ihgd", probs_ahead, value_heads, preferred_element_type=jnp.float32
    )
    mixed_ahead = mixed_ahead.astype(jnp.bfloat16).reshape(queries_ahead.shape)
    forward_sum = contract_last(mixed_ahead, w_out)
    queries_back = project(back_full, w_query)
    keys_back = project(back_full, w_key)
    values_back = project(back_full, w_value)
    query_back_heads, key_back_heads, unused_values = split_heads(
        queries_back, keys_back, values_back, kv_local
    )
    probs_back = attend_probs(query_back_heads, key_back_heads, allowed(doc_ids[0, 0, 1]))
    dmixed = jnp.dot(grad_full, w_out, preferred_element_type=jnp.float32).astype(jnp.bfloat16)
    dqueries, dkeys, dvalues = attend_back(
        dmixed, queries_back, keys_back, values_back, probs_back, kv_local
    )
    dkey_cols = dkeys.astype(jnp.bfloat16)
    dvalue_cols = dvalues.astype(jnp.bfloat16)
    dnormed = (
        contract_last(dqueries, w_query)
        + contract_last(dkey_cols, w_key)
        + contract_last(dvalue_cols, w_value)
    )
    forward_share, backward_share = (
        lax.psum_scatter(
            forward_sum.astype(jnp.bfloat16), "tp", scatter_dimension=0, tiled=True
        ).astype(jnp.float32),
        lax.psum_scatter(
            dnormed.astype(jnp.bfloat16), "tp", scatter_dimension=0, tiled=True
        ).astype(jnp.float32),
    )
    outgoing = (forward_rows.astype(jnp.float32) + forward_share).astype(jnp.bfloat16)
    scaled = backward_rows.astype(jnp.float32) * inverse_back
    grad_back = (
        grad_rows.astype(jnp.float32)
        + inverse_back
        * (backward_share - scaled * jnp.mean(backward_share * scaled, axis=-1, keepdims=True))
    ).astype(jnp.bfloat16)
    act_out = handoff(outgoing, 1)[None, None]
    grad_out = handoff(grad_back, -1)[None, None]
    copies = lax.axis_size("dp")
    normed_cols = lax.all_to_all(back_full, "dp", split_axis=1, concat_axis=0, tiled=True)
    all_queries, all_keys, all_values = (
        lax.all_gather(dqueries, "dp", axis=0, tiled=True),
        lax.all_gather(dkey_cols, "dp", axis=0, tiled=True),
        lax.all_gather(dvalue_cols, "dp", axis=0, tiled=True),
    )
    grad_query = per_copy(normed_cols, all_queries, copies)[None]
    grad_key = per_copy(normed_cols, all_keys, copies)[None]
    grad_value = per_copy(normed_cols, all_values, copies)[None]
    return (act_out, grad_out, grad_query, grad_key, grad_value)


def solution(mesh):
    placed = (
        P("pp", "dp", "tp", None),
        P("pp", "dp", "tp", None),
        P("pp", "dp", "tp", None),
        P("pp", "dp", None, None),
        P("pp", None, "tp"),
        P("pp", None, "tp"),
        P("pp", None, "tp"),
        P("pp", None, "tp"),
    )
    return jax.shard_map(
        body,
        mesh=mesh,
        in_specs=placed,
        out_specs=(
            P("pp", "dp", "tp", None),
            P("pp", "dp", "tp", None),
            P("pp", "dp", "tp"),
            P("pp", "dp", "tp"),
            P("pp", "dp", "tp"),
        ),
        check_vma=False,
    )
```

profile of v0, /device:TPU:1, one launch (start us, length us, event | category | flops | bytes accessed | tf_op | source)
XLA Modules:
  0.0 207.6 jit_solution(1931874249272098279)
XLA Ops:
  7.2 0.0 all-gather.7.cloned.1.call-start
  7.2 1.2 fusion.81
  8.5 0.6 copy-done.12
  9.1 1.8 fusion.76
  10.9 0.0 all-gather.9.cloned.1.call-start
  10.9 0.7 all-gather.9.cloned.1.call-update
  11.6 0.0 all-gather.5.cloned.1.call-start
  11.7 1.1 fusion.82
  12.8 1.8 fusion.83
  14.6 0.7 fusion.90
  15.3 0.1 fusion.91
  15.4 25.2 %all-gather.7.cloned.1.call-done = bf16[128,4096]{1,0:T(8,128)(2,1)} async-done(((bf16[32,4096]{1,0:T(8,128)(2,1)}), bf16[128,4096]{1,0:T(8,128)(2,1)}) %all-gather.7.cloned.1.call-update) | async-done | bytes 1048592 | tf_op jit(solution)/shard_map/all_gather | solution.py:104
  40.6 5.0 %fusion.42 = bf16[128,1024]{1,0:T(8,128)(2,1)S(1)} fusion(bf16[128,4096]{1,0:T(8,128)(2,1)} %all-gather.7.cloned.1.call-done, bf16[1,4096,1024]{2,1,0:T(8,128)(2,1)} %param.12), kind=kOutput, calls=%fused_computation.49 | convolution fusion | flops 1073872896 | bytes 9699328 | tf_op jit(solution)/shard_map/dot_general | solution.py:30
  45.6 0.8 copy.52
  46.5 0.4 fusion.57
  47.0 0.1 copy.36
  47.1 2.0 fusion.51
  49.2 20.4 %all-gather.9.cloned.1.call-done = bf16[1,1,128,4096]{3,2,1,0:T(8,128)(2,1)} async-done(((bf16[1,1,32,4096]{3,2,1,0:T(8,128)(2,1)}), bf16[1,1,128,4096]{3,2,1,0:T(8,128)(2,1)}) %all-gather.9.cloned.1.call-update) | async-done | bytes 1048592 | tf_op jit(solution)/shard_map/all_gather | solution.py:105
  69.6 5.7 %fusion.45 = bf16[128,1024]{1,0:T(8,128)(2,1)} fusion(bf16[1,4096,1024]{2,1,0:T(8,128)(2,1)} %param.15, bf16[1,1,128,4096]{3,2,1,0:T(8,128)(2,1)} %all-gather.9.cloned.1.call-done), kind=kOutput, calls=%fused_computation.50 | convolution fusion | flops 1073872896 | bytes 9699328 | tf_op jit(solution)/shard_map/dot_general | solution.py:130
  75.3 1.1 copy.53
  76.4 2.7 %fusion.111 = (f32[2,4,128]{2,1,0:T(4,128)}, f32[2,4,128,128]{2,3,1,0:T(8,128)}) fusion(bf16[128,2,128,1]{0,2,3,1:T(8,128)(2,1)S(1)} %copy.36, bf16[128,2,4,128]{0,3,2,1:T(8,128)(2,1)} %bitcast.170, pred[128,128]{0,1:T(8,128)(4,1)} %fusion.90), kind=kOutput, calls=%fused_computation.113 | convolution fusion | flops 34078848 | bytes 872448 | tf_op jit(solution)/shard_map/sub | solution.py:55
  79.1 1.8 divide_convert_fusion
  80.9 1.0 convolution_bitcast_fusion
  81.9 2.5 %convolution_convert_fusion.3 = bf16[2,128,4,128]{3,1,2,0:T(8,128)(2,1)} fusion(bf16[128,2,128,1]{0,2,3,1:T(8,128)(2,1)S(1)} %copy.36, f32[2,4,128,128]{2,3,1,0:T(8,128)} %convolution_bitcast_fusion, bf16[2,4,128,128]{2,3,1,0:T(8,128)(2,1)} %divide_convert_fusion), kind=kOutput, calls=%fused_computation.51 | convolution fusion | flops 34604160 | bytes 1114112 | tf_op jit(solution)/shard_map/hgij,jhd->ihgd/dot_general | solution.py:69
  84.4 2.4 %fusion.60 = bf16[2,128,128]{2,1,0:T(8,128)(2,1)} fusion(bf16[128,2,4,128]{0,3,2,1:T(8,128)(2,1)} %bitcast.171, f32[2,4,128,128]{2,3,1,0:T(8,128)} %convolution_bitcast_fusion, bf16[2,4,128,128]{2,3,1,0:T(8,128)(2,1)} %divide_convert_fusion), kind=kOutput, calls=%fused_computation.59 | convolution fusion | flops 34505856 | bytes 1114112 | tf_op jit(solution)/shard_map/hgij,ihgd->jhd/dot_general | solution.py:70
  86.9 9.4 %all_gather.21 = bf16[256,1024]{0,1:T(8,128)(2,1)} all-gather(bf16[128,1024]{0,1:T(8,128)(2,1)} %bitcast.161), channel_id=1, replica_groups=mesh['pp'=4,'tp'=4,'dp'=2] {'dp'}, dimensions={0}, use_global_device_ids=true | all-gather | bytes 786432 | tf_op jit(solution)/shard_map/all_gather | solution.py:161
  96.2 2.0 copy.28
  98.3 1.3 copy.51
  99.6 3.6 %all-to-all-start = ((bf16[128,2,2048]{0,2,1:T(8,128)(2,1)}), bf16[128,2,2048]{0,2,1:T(8,128)(2,1)S(1)}, u32[]{:S(2)}, u32[]{:S(2)}) async-start(bf16[128,2,2048]{0,2,1:T(8,128)(2,1)} %bitcast.155), calls=%async_computation.2 | async-start | bytes 2097152 | tf_op jit(solution)/shard_map/all_to_all | solution.py:159
  103.2 0.0 reduce-scatter.5.cloned.1.call-start
  103.2 13.3 %all_gather.22 = bf16[256,256]{0,1:T(8,128)(2,1)S(1)} all-gather(bf16[128,256]{0,1:T(8,128)(2,1)} %bitcast.167), channel_id=1, replica_groups=mesh['pp'=4,'tp'=4,'dp'=2] {'dp'}, dimensions={0}, use_global_device_ids=true | all-gather | bytes 196608 | tf_op jit(solution)/shard_map/all_gather | solution.py:162
  116.5 0.8 copy.29
  117.3 1.2 fusion.61
  118.5 3.8 %all_gather.23 = bf16[256,256]{0,1:T(8,128)(2,1)S(1)} all-gather(bf16[128,256]{0,1:T(8,128)(2,1)S(1)} %bitcast.163), channel_id=1, replica_groups=mesh['pp'=4,'tp'=4,'dp'=2] {'dp'}, dimensions={0}, use_global_device_ids=true | all-gather | bytes 196608 | tf_op jit(solution)/shard_map/all_gather | solution.py:163
  122.3 0.8 copy.30
  123.0 6.4 %fusion.7 = f32[128,4096]{1,0:T(8,128)S(1)} fusion(bf16[128,1024]{0,1:T(8,128)(2,1)} %bitcast.162, bf16[1,4096,1024]{2,1,0:T(8,128)(2,1)} %param.12), kind=kOutput, calls=%fused_computation.8 | convolution fusion | flops 1073741824 | bytes 10747904 | tf_op jit(solution)/shard_map/dot_general | solution.py:34
  129.5 0.8 convolution_add_fusion.1
  130.3 0.7 copy-done.2
  131.1 1.8 fusion.13
  132.9 0.2 reduce-scatter.3.cloned.1.call-start
  133.1 0.0 all-gather.5.cloned.1.call-done
  133.2 5.0 %fusion.39 = bf16[128,1024]{1,0:T(8,128)(2,1)S(1)} fusion(bf16[128,4096]{1,0:T(8,128)(2,1)} %all-gather.5.cloned.1.call-done, bf16[1,4096,1024]{2,1,0:T(8,128)(2,1)} %param.12), kind=kOutput, calls=%fused_computation.48 | convolution fusion | flops 1073872896 | bytes 9699328 | tf_op jit(solution)/shard_map/dot_general | solution.py:30
  138.1 0.9 reshape.96
  139.0 1.7 fusion.54
  140.7 2.6 %fusion.48 = bf16[128,256]{1,0:T(8,128)(2,1)S(1)} fusion(bf16[128,4096]{1,0:T(8,128)(2,1)} %all-gather.5.cloned.1.call-done, bf16[1,4096,256]{2,1,0:T(8,128)(2,1)} %param.14), kind=kOutput, calls=%fused_computation.55 | convolution fusion | flops 268468224 | bytes 3211264 | tf_op jit(solution)/shard_map/dot_general | solution.py:30
  143.3 0.7 copy.42
  144.0 0.9 fusion.106
  144.9 1.0 fusion.37
  146.0 1.5 convolution_convert_fusion.4
  147.5 7.3 %fusion.14 = bf16[128,4096]{1,0:T(8,128)(2,1)} fusion(bf16[128,1024]{0,1:T(8,128)(2,1)S(1)} %bitcast.169, bf16[1,4096,1024]{2,1,0:T(8,128)(2,1)} %param.15), kind=kOutput, calls=%fused_computation.18 | convolution fusion | flops 1074266112 | bytes 9699328 | tf_op jit(solution)/shard_map/dot_general | solution.py:34
  154.9 6.6 %convolution_convert_fusion = bf16[2,2048,1024]{2,1,0:T(8,128)(2,1)} fusion(bf16[2,128,1024]{2,1,0:T(8,128)(2,1)} %bitcast.158, bf16[128,2,2048]{0,2,1:T(8,128)(2,1)S(1)} %all-to-all-done), kind=kOutput, calls=%fused_computation.14 | convolution fusion | flops 1077936128 | bytes 9961472 | tf_op jit(solution)/shard_map/nsd,nse->nde/dot_general | solution.py:85
  161.5 2.0 convolution_convert_fusion.2
  163.5 2.1 %convolution_convert_fusion.1 = bf16[2,2048,256]{2,1,0:T(8,128)(2,1)} fusion(bf16[2,128,256]{2,1,0:T(8,128)(2,1)S(1)} %bitcast.166, bf16[128,2,2048]{0,2,1:T(8,128)(2,1)S(1)} %all-to-all-done), kind=kOutput, calls=%fused_computation.21 | convolution fusion | flops 269484032 | bytes 3276800 | tf_op jit(solution)/shard_map/nsd,nse->nde/dot_general | solution.py:85
  165.6 10.0 %convert_reduce_fusion = f32[2048,1024]{1,0:T(8,128)} fusion(bf16[2,2048,1024]{2,1,0:T(8,128)(2,1)} %convolution_convert_fusion), kind=kLoop, calls=%fused_computation.3 | loop fusion | flops 6291456 | bytes 16777216 | tf_op jit(solution)/shard_map/reduce_sum | solution.py:92
  175.6 1.2 fusion.80
  176.9 1.2 fusion.79
  178.0 3.9 %collective-permute-start.1 = (bf16[32,4096]{1,0:T(8,128)(2,1)S(1)}, bf16[32,4096]{1,0:T(8,128)(2,1)S(1)}, u32[]{:S(2)}, u32[]{:S(2)}) collective-permute-start(bf16[32,4096]{1,0:T(8,128)(2,1)S(1)} %fusion.79), channel_id=1, source_target_pairs={{0,24},{8,0},{16,8},{24,16},{1,25},{9,1},{17,9},{25,17},{2,26},{10... | collective-permute-start | bytes 786440 | tf_op jit(solution)/shard_map/ppermute | solution.py:14
  181.9 9.3 %reduce-scatter.3.cloned.1.call-done = bf16[32,4096]{1,0:T(8,128)(2,1)} async-done(((bf16[128,4096]{1,0:T(8,128)(2,1)}), bf16[32,4096]{1,0:T(8,128)(2,1)}) %reduce-scatter.3.cloned.1.call-update) | async-done | bytes 262160 | tf_op jit(solution)/shard_map/reduce_scatter | solution.py:142
  191.2 1.0 fusion.84
  192.2 2.2 %collective-permute-start = (bf16[32,4096]{1,0:T(8,128)(2,1)S(1)}, bf16[32,4096]{1,0:T(8,128)(2,1)S(1)}, u32[]{:S(2)}, u32[]{:S(2)}) collective-permute-start(bf16[32,4096]{1,0:T(8,128)(2,1)S(1)} %fusion.84), channel_id=1, source_target_pairs={{0,8},{8,16},{16,24},{24,0},{1,9},{9,17},{17,25},{25,1},{2,10},{10... | collective-permute-start | bytes 786440 | tf_op jit(solution)/shard_map/ppermute | solution.py:14
  194.4 3.5 %convert_reduce_fusion.2 = f32[2048,256]{1,0:T(8,128)} fusion(bf16[2,2048,256]{2,1,0:T(8,128)(2,1)} %convolution_convert_fusion.2), kind=kLoop, calls=%fused_computation.20 | loop fusion | flops 1572864 | bytes 4194304 | tf_op jit(solution)/shard_map/reduce_sum | solution.py:92
  197.9 1.7 convert_reduce_fusion.1
  199.6 0.7 copy.70
  200.3 0.7 copy.71
  (43 shorter events, 0.2 us)
Async XLA Ops:
  7.2 39.3 %copy-start = (bf16[1,4096,256]{2,1,0:T(8,128)(2,1)S(1)}, bf16[1,4096,256]{2,1,0:T(8,128)(2,1)}, u32[]{:S(2)}) copy-start(bf16[1,4096,256]{2,1,0:T(8,128)(2,1)} %param.13) | copy-start | bytes 6291460
  7.2 7.4 %copy-start.14 = (s32[1,1,2,128]{3,2,1,0:T(2,128)S(1)}, s32[1,1,2,128]{3,2,1,0:T(2,128)}, u32[]{:S(2)}) copy-start(s32[1,1,2,128]{3,2,1,0:T(2,128)} %param.11) | copy-start | bytes 3076
  7.2 33.4 %all-gather.7.cloned.1.call-start = ((), (), s32[]{:S(2)}) async-start(), calls=%async_computation.5 | async-start | bytes 1310720 | tf_op jit(solution)/shard_map/all_gather | solution.py:104
  8.5 0.6 copy-start.12
  10.9 58.7 %all-gather.9.cloned.1.call-start = ((), (), s32[]{:S(2)}) async-start(), calls=%async_computation.7 | async-start | bytes 1310720 | tf_op jit(solution)/shard_map/all_gather | solution.py:105
  11.6 121.5 %all-gather.5.cloned.1.call-start = ((), (), s32[]{:S(2)}) async-start(), calls=%async_computation.3 | async-start | bytes 1310720 | tf_op jit(solution)/shard_map/all_gather | solution.py:103
  40.6 5.9 %copy-start.1 = (bf16[128,4096]{1,0:T(8,128)(2,1)S(1)}, bf16[128,4096]{1,0:T(8,128)(2,1)}, u32[]{:S(2)}) copy-start(bf16[128,4096]{1,0:T(8,128)(2,1)} %all-gather.7.cloned.1.call-done) | copy-start | bytes 3145732
  99.6 55.3 %all-to-all-start = ((bf16[128,2,2048]{0,2,1:T(8,128)(2,1)}), bf16[128,2,2048]{0,2,1:T(8,128)(2,1)S(1)}, u32[]{:S(2)}, u32[]{:S(2)}) async-start(bf16[128,2,2048]{0,2,1:T(8,128)(2,1)} %bitcast.155), calls=%async_computation.2 | async-start | bytes 2097152 | tf_op jit(solution)/shard_map/all_to_all | solution.py:159
  103.2 72.5 %reduce-scatter.5.cloned.1.call-start = ((), (), s32[]{:S(2)}) async-start(), calls=%async_computation.6 | async-start | bytes 1310720 | tf_op jit(solution)/shard_map/reduce_scatter | solution.py:145
  123.0 6.4 %copy-start.10 = (bf16[2,128,128]{2,1,0:T(8,128)(2,1)S(1)}, bf16[2,128,128]{2,1,0:T(8,128)(2,1)}, u32[]{:S(2)}) copy-start(bf16[2,128,128]{2,1,0:T(8,128)(2,1)} %fusion.60) | copy-start | bytes 196612
  129.5 1.6 copy-start.2
  132.9 58.3 %reduce-scatter.3.cloned.1.call-start = ((), (), s32[]{:S(2)}) async-start(), calls=%async_computation.4 | async-start | bytes 1310720 | tf_op jit(solution)/shard_map/reduce_scatter | solution.py:142
  140.7 3.3 %copy-start.7 = (bf16[128,2,4,128]{3,2,1,0:T(4,128)(2,1)S(1)}, bf16[128,2,4,128]{3,2,1,0:T(4,128)(2,1)}, u32[]{:S(2)}) copy-start(bf16[128,2,4,128]{3,2,1,0:T(4,128)(2,1)} %reshape.96) | copy-start | bytes 786436
  144.0 2.0 copy-start.11
  154.8 6.6 %copy-start.8 = (bf16[256,256]{1,0:T(8,128)(2,1)S(1)}, bf16[256,256]{1,0:T(8,128)(2,1)}, u32[]{:S(2)}) copy-start(bf16[256,256]{1,0:T(8,128)(2,1)} %copy.29) | copy-start | bytes 393220
  161.5 2.0 copy-start.9
  165.6 10.0 %copy-start.4 = (bf16[1,1,32,4096]{3,2,1,0:T(8,128)(2,1)S(1)}, bf16[1,1,32,4096]{3,2,1,0:T(8,128)(2,1)}, u32[]{:S(2)}) copy-start(bf16[1,1,32,4096]{3,2,1,0:T(8,128)(2,1)} %param.9) | copy-start | bytes 786436
  165.6 10.0 %copy-start.13 = (f32[32]{0:T(128)S(1)}, f32[32]{0:T(128)}, u32[]{:S(2)}) copy-start(f32[32]{0:T(128)} %copy-done.12) | copy-start | bytes 388
  165.6 11.3 %copy-start.6 = (bf16[1,1,32,4096]{3,2,1,0:T(8,128)(2,1)S(1)}, bf16[1,1,32,4096]{3,2,1,0:T(8,128)(2,1)}, u32[]{:S(2)}) copy-start(bf16[1,1,32,4096]{3,2,1,0:T(8,128)(2,1)} %param.10) | copy-start | bytes 786436
  165.6 25.6 %copy-start.5 = (bf16[1,1,32,4096]{3,2,1,0:T(8,128)(2,1)S(1)}, bf16[1,1,32,4096]{3,2,1,0:T(8,128)(2,1)}, u32[]{:S(2)}) copy-start(bf16[1,1,32,4096]{3,2,1,0:T(8,128)(2,1)} %param.8) | copy-start | bytes 786436
  178.0 21.6 %collective-permute-start.1 = (bf16[32,4096]{1,0:T(8,128)(2,1)S(1)}, bf16[32,4096]{1,0:T(8,128)(2,1)S(1)}, u32[]{:S(2)}, u32[]{:S(2)}) collective-permute-start(bf16[32,4096]{1,0:T(8,128)(2,1)S(1)} %fusion.79), channel_id=1, source_target_pairs={{0,24},{8,0},{16,8},{24,16},{1,25},{9,1},{17,9},{25,17},{2,26},{10... | collective-permute-start | bytes 786440 | tf_op jit(solution)/shard_map/ppermute | solution.py:14
  192.2 5.7 %copy-start.3 = (bf16[2,2048,256]{2,1,0:T(8,128)(2,1)S(1)}, bf16[2,2048,256]{2,1,0:T(8,128)(2,1)}, u32[]{:S(2)}) copy-start(bf16[2,2048,256]{2,1,0:T(8,128)(2,1)} %convolution_convert_fusion.1) | copy-start | bytes 6291460
  192.2 7.4 %collective-permute-start = (bf16[32,4096]{1,0:T(8,128)(2,1)S(1)}, bf16[32,4096]{1,0:T(8,128)(2,1)S(1)}, u32[]{:S(2)}, u32[]{:S(2)}) collective-permute-start(bf16[32,4096]{1,0:T(8,128)(2,1)S(1)} %fusion.84), channel_id=1, source_target_pairs={{0,8},{8,16},{16,24},{24,0},{1,9},{9,17},{17,25},{25,1},{2,10},{10... | collective-permute-start | bytes 786440 | tf_op jit(solution)/shard_map/ppermute | solution.py:14
Sparse Core Ops, SparseCore 0:
  11.0 29.5 all-gather.6
  42.2 27.4 all-gather.8
  71.8 27.2 all-gather.4
  133.0 29.5 reduce-scatter.4
  165.4 25.7 reduce-scatter.2
where the time goes:
time: 209 us; the launch traced here: 208 us
  matrix products  62.8 us (30%)
  waiting for transfers between devices  55.7 us (27%)
  other arithmetic  27.1 us (13%)
  blocking collectives  26.5 us (13%)
  between operations  14 us (7%)
  local copies, waits for them, and re-layouts  11.4 us (5%)
  starting transfers between devices  10 us (5%)
    all_gather x1, waiting for transfers between devices, body(): lax.all_gather(normed_back, 'tp', axis=0, tiled=True)  25.2 us
    all_gather x1, waiting for transfers between devices, body(): lax.all_gather(grad_rows, 'tp', axis=0, tiled=True)  20.4 us
    dot_general x6, matrix products, project(): jnp.dot(normed, weight, preferred_element_type=jnp.float32)  16.7 us
    dot_general x4, matrix products, contract_last(): lax.dot_general(left_side, right_side, (((1,), (1,)), ((), ())), preferre...  16.4 us
    reduce_sum x3, other arithmetic, per_copy(): return jnp.sum(kept.astype(jnp.float32), axis=0)  15.2 us
    all_gather x1, blocking collectives, body(): lax.all_gather(dkey_cols, 'dp', axis=0, tiled=True)  13.3 us
    dot_general x3, matrix products, per_copy(): jnp.einsum('nsd,nse->nde', left_side.reshape(copies, length, left_side.sh...  10.7 us
    all_gather x1, blocking collectives, body(): lax.all_gather(dqueries, 'dp', axis=0, tiled=True)  9.38 us
  transfers between devices with their start and end apart: 8, of which 3 were waited for; matrix products, arithmetic and copies ran while one was open for 46% of the time, Pallas kernels for 0%

commit v1 on v0

--- a/solution.py
+++ b/solution.py
@@ -101,7 +101,9 @@
     normed_back, inverse_back = norm_rows(backward_rows)
     ahead_full, back_full, grad_full = (
         lax.all_gather(normed_ahead, "tp", axis=0, tiled=True),
-        lax.all_gather(normed_back, "tp", axis=0, tiled=True),
+        jnp.concatenate(
+            lax.all_to_all(jnp.stack([normed_back] * lax.axis_size("tp")), "tp", 0, 0), axis=0
+        ),
         lax.all_gather(grad_rows, "tp", axis=0, tiled=True),
     )
     w_query = query_weight[0]

time: 209 us -> 213 us (1.019)
  waiting for transfers between devices: 55.7 us -> 43.6 us
  local copies, waits for them, and re-layouts: 11.4 us -> 20.6 us
  starting transfers between devices: 10 us -> 15.7 us
  matrix products: 62.8 us -> 67.5 us
  other arithmetic: 27.1 us -> 24.4 us
    all_to_all x0 -> x1, waiting for transfers between devices: none -> 40.3 us  [body(): lax.all_to_all(jnp.stack([normed_back] * lax.axis_size('tp')), 'tp', 0, 0)]
    all_gather x1 -> x0, waiting for transfers between devices: 25.2 us -> none  [body(): lax.all_gather(normed_back, 'tp', axis=0, tiled=True)]
    all_gather x1, waiting for transfers between devices: 20.4 us -> 0.02 us  [body(): lax.all_gather(grad_rows, 'tp', axis=0, tiled=True)]
    reduce_scatter x1, waiting for transfers between devices: 9.31 us -> 2.55 us  [body(): lax.psum_scatter(forward_sum.astype(jnp.bfloat16), 'tp', scatter_dimensio...]
    all_to_all x0 -> x1, starting transfers between devices: none -> 5.41 us  [body(): lax.all_to_all(jnp.stack([normed_back] * lax.axis_size('tp')), 'tp', 0, 0)]
    all_to_all x1 -> x2, local copies, waits for them, and re-layouts: 1.3 us -> 5.23 us  [body(): lax.all_to_all(back_full, 'dp', split_axis=1, concat_axis=0, tiled=True)]
  transfers between devices with their start and end apart: 8 -> 8, of which waited for: 3 -> 2; matrix products, arithmetic and copies ran while one was open for 46% -> 51% of each run, Pallas kernels for 0% -> 0%
where the time goes in v1:
time: 213 us; the launch traced here: 212 us
  matrix products  67.5 us (32%)
  waiting for transfers between devices  43.6 us (20%)
  blocking collectives  26.3 us (12%)
  other arithmetic  24.4 us (11%)
  local copies, waits for them, and re-layouts  20.6 us (10%)
  starting transfers between devices  15.7 us (7%)
  between operations  14 us (7%)
    all_to_all x1, waiting for transfers between devices, body(): lax.all_to_all(jnp.stack([normed_back] * lax.axis_size('tp')), 'tp', 0, 0)  40.3 us
    dot_general x6, matrix products, project(): jnp.dot(normed, weight, preferred_element_type=jnp.float32)  17.6 us
    dot_general x4, matrix products, contract_last(): lax.dot_general(left_side, right_side, (((1,), (1,)), ((), ())), preferre...  16.5 us
    reduce_sum x3, other arithmetic, per_copy(): return jnp.sum(kept.astype(jnp.float32), axis=0)  15.2 us
    all_gather x1, blocking collectives, body(): lax.all_gather(dkey_cols, 'dp', axis=0, tiled=True)  13.1 us
    dot_general x3, matrix products, per_copy(): jnp.einsum('nsd,nse->nde', left_side.reshape(copies, length, left_side.sh...  10.7 us
    all_gather x1, blocking collectives, body(): lax.all_gather(dqueries, 'dp', axis=0, tiled=True)  9.25 us
    ppermute x2, starting transfers between devices, from_behind(): return lax.ppermute(value, axis, pairs)  6.44 us
  transfers between devices with their start and end apart: 8, of which 2 were waited for; matrix products, arithmetic and copies ran while one was open for 51% of the time, Pallas kernels for 0%

profile of v1, /device:TPU:1, one launch (start us, length us, event | category | flops | bytes accessed | tf_op | source)
XLA Modules:
  0.0 212.1 jit_solution(9827720500313551606)
XLA Ops:
  7.2 0.0 all-gather.6.cloned.1.call-start
  7.2 0.7 all-gather.6.cloned.1.call-update
  7.9 1.2 fusion.81
  9.1 0.6 copy-done.11
  9.7 1.1 fusion.76
  10.8 1.1 stack.2
  11.8 5.4 %all-to-all-start = ((bf16[4,32,4096]{2,1,0:T(8,128)(2,1)}), bf16[4,32,4096]{2,1,0:T(8,128)(2,1)S(1)}, u32[]{:S(2)}, u32[]{:S(2)}) async-start(bf16[4,32,4096]{2,1,0:T(8,128)(2,1)} %stack.2), calls=%async_computation.1 | async-start | bytes 2097152 | tf_op jit(solution)/shard_map/all_to_all | solution.py:105
  17.2 0.2 fusion.82
  17.4 0.8 fusion.83
  18.3 0.7 fusion.90
  19.0 0.1 fusion.91
  19.1 40.3 %all-to-all-done = bf16[4,32,4096]{2,1,0:T(8,128)(2,1)S(1)} async-done(((bf16[4,32,4096]{2,1,0:T(8,128)(2,1)}), bf16[4,32,4096]{2,1,0:T(8,128)(2,1)S(1)}, u32[]{:S(2)}, u32[]{:S(2)}) %all-to-all-start) | async-done | bytes 1048608 | tf_op jit(solution)/shard_map/all_to_all | solution.py:105
  59.4 5.3 %fusion.42 = bf16[128,1024]{1,0:T(8,128)(2,1)} fusion(bf16[128,4096]{1,0:T(8,128)(2,1)S(1)} %bitcast.154, bf16[1,4096,1024]{2,1,0:T(8,128)(2,1)} %param.12), kind=kOutput, calls=%fused_computation.49 | convolution fusion | flops 1073872896 | bytes 9699328 | tf_op jit(solution)/shard_map/dot_general | solution.py:30
  64.7 1.8 copy.69
  66.5 0.4 fusion.57
  67.0 0.7 copy.54
  67.7 2.1 fusion.51
  69.9 0.0 all-gather.6.cloned.1.call-done
  69.9 5.7 %fusion.45 = bf16[128,1024]{1,0:T(8,128)(2,1)} fusion(bf16[1,4096,1024]{2,1,0:T(8,128)(2,1)} %param.15, bf16[1,1,128,4096]{3,2,1,0:T(8,128)(2,1)} %all-gather.6.cloned.1.call-done), kind=kOutput, calls=%fused_computation.50 | convolution fusion | flops 1073872896 | bytes 9699328 | tf_op jit(solution)/shard_map/dot_general | solution.py:132
  75.6 1.8 copy.70
  77.4 2.7 %fusion.111 = (f32[2,4,128]{2,1,0:T(4,128)}, f32[2,4,128,128]{2,3,1,0:T(8,128)}) fusion(bf16[128,2,128,1]{0,2,3,1:T(8,128)(2,1)S(1)} %copy-done.9, bf16[128,2,4,128]{0,3,2,1:T(8,128)(2,1)} %bitcast.172, pred[128,128]{0,1:T(8,128)(4,1)} %fusion.90), kind=kOutput, calls=%fused_computation.113 | convolution fusion | flops 34078848 | bytes 872448 | tf_op jit(solution)/shard_map/sub | solution.py:55
  80.1 1.8 divide_convert_fusion
  81.9 2.0 convolution_bitcast_fusion
  83.8 2.5 %fusion.60 = bf16[2,128,128]{2,1,0:T(8,128)(2,1)} fusion(bf16[128,2,4,128]{0,3,2,1:T(8,128)(2,1)} %bitcast.173, f32[2,4,128,128]{2,3,1,0:T(8,128)} %convolution_bitcast_fusion, bf16[2,4,128,128]{2,3,1,0:T(8,128)(2,1)} %divide_convert_fusion), kind=kOutput, calls=%fused_computation.59 | convolution fusion | flops 34505856 | bytes 1114112 | tf_op jit(solution)/shard_map/hgij,ihgd->jhd/dot_general | solution.py:70
  86.3 2.5 %convolution_convert_fusion.3 = bf16[2,128,4,128]{3,1,2,0:T(8,128)(2,1)} fusion(bf16[128,2,128,1]{0,2,3,1:T(8,128)(2,1)S(1)} %copy-done.9, f32[2,4,128,128]{2,3,1,0:T(8,128)} %convolution_bitcast_fusion, bf16[2,4,128,128]{2,3,1,0:T(8,128)(2,1)} %divide_convert_fusion), kind=kOutput, calls=%fused_computation.51 | convolution fusion | flops 34604160 | bytes 1114112 | tf_op jit(solution)/shard_map/hgij,jhd->ihgd/dot_general | solution.py:69
  88.8 9.2 %all_gather.17 = bf16[256,1024]{0,1:T(8,128)(2,1)} all-gather(bf16[128,1024]{0,1:T(8,128)(2,1)} %bitcast.163), channel_id=1, replica_groups=mesh['pp'=4,'tp'=4,'dp'=2] {'dp'}, dimensions={0}, use_global_device_ids=true | all-gather | bytes 786432 | tf_op jit(solution)/shard_map/all_gather | solution.py:163
  98.1 2.1 copy.46
  100.2 1.6 all_to_all.16
  101.7 3.7 %copy.45 = bf16[128,2,2048]{0,2,1:T(8,128)(2,1)} copy(bf16[128,2,2048]{2,1,0:T(2,128)(2,1)} %all_to_all.16) | data formatting | bytes 2097152 | tf_op jit(solution)/shard_map/all_to_all | solution.py:161
  105.4 3.6 %all-to-all-start.1 = ((bf16[128,2,2048]{0,2,1:T(8,128)(2,1)}), bf16[128,2,2048]{0,2,1:T(8,128)(2,1)S(1)}, u32[]{:S(2)}, u32[]{:S(2)}) async-start(bf16[128,2,2048]{0,2,1:T(8,128)(2,1)} %copy.45), calls=%async_computation.3 | async-start | bytes 2097152 | tf_op jit(solution)/shard_map/all_to_all | solution.py:161
  109.0 0.0 reduce-scatter.5.cloned.1.call-start
  109.0 13.1 %all_gather.18 = bf16[256,256]{0,1:T(8,128)(2,1)S(1)} all-gather(bf16[128,256]{0,1:T(8,128)(2,1)} %bitcast.169), channel_id=1, replica_groups=mesh['pp'=4,'tp'=4,'dp'=2] {'dp'}, dimensions={0}, use_global_device_ids=true | all-gather | bytes 196608 | tf_op jit(solution)/shard_map/all_gather | solution.py:164
  122.1 0.8 copy.47
  122.9 1.2 fusion.61
  124.1 3.9 %all_gather.19 = bf16[256,256]{0,1:T(8,128)(2,1)} all-gather(bf16[128,256]{0,1:T(8,128)(2,1)S(1)} %bitcast.165), channel_id=1, replica_groups=mesh['pp'=4,'tp'=4,'dp'=2] {'dp'}, dimensions={0}, use_global_device_ids=true | all-gather | bytes 196608 | tf_op jit(solution)/shard_map/all_gather | solution.py:165
  128.1 1.7 copy.48
  129.7 6.4 %fusion.7 = f32[128,4096]{1,0:T(8,128)S(1)} fusion(bf16[128,1024]{0,1:T(8,128)(2,1)} %bitcast.164, bf16[1,4096,1024]{2,1,0:T(8,128)(2,1)} %param.12), kind=kOutput, calls=%fused_computation.8 | convolution fusion | flops 1073741824 | bytes 10747904 | tf_op jit(solution)/shard_map/dot_general | solution.py:34
  136.2 0.8 convolution_add_fusion.1
  137.0 0.7 copy-done.1
  137.8 1.8 fusion.13
  139.6 0.2 reduce-scatter.3.cloned.1.call-start
  139.9 5.7 %fusion.39 = bf16[128,1024]{1,0:T(8,128)(2,1)} fusion(bf16[128,4096]{1,0:T(8,128)(2,1)} %all-gather.4.cloned.1.call-done, bf16[1,4096,1024]{2,1,0:T(8,128)(2,1)} %param.12), kind=kOutput, calls=%fused_computation.48 | convolution fusion | flops 1073872896 | bytes 9699328 | tf_op jit(solution)/shard_map/dot_general | solution.py:30
  145.5 1.8 reshape.109
  147.4 1.7 fusion.54
  149.1 2.4 %fusion.48 = bf16[128,256]{1,0:T(8,128)(2,1)S(1)} fusion(bf16[128,4096]{1,0:T(8,128)(2,1)} %all-gather.4.cloned.1.call-done, bf16[1,4096,256]{2,1,0:T(8,128)(2,1)} %param.14), kind=kOutput, calls=%fused_computation.55 | convolution fusion | flops 268468224 | bytes 3211264 | tf_op jit(solution)/shard_map/dot_general | solution.py:30
  151.4 0.7 copy.60
  152.2 1.9 fusion.106
  154.1 2.0 fusion.37
  156.1 2.3 %convolution_convert_fusion.4 = bf16[2,128,4,128]{3,1,2,0:T(8,128)(2,1)} fusion(bf16[128,2,128,1]{0,2,3,1:T(8,128)(2,1)S(1)} %bitcast.180, f32[2,4,128]{2,1,0:T(4,128)} %fusion.106, f32[2,4,128,128]{2,3,1,0:T(8,128)} %fusion.37), kind=kOutput, calls=%fused_computation.52 | convolution fusion | flops 34079872 | bytes 856064 | tf_op jit(solution)/shard_map/hgij,jhd->ihgd/dot_general | solution.py:120
  158.3 7.4 %fusion.14 = bf16[128,4096]{1,0:T(8,128)(2,1)} fusion(bf16[128,1024]{0,1:T(8,128)(2,1)} %bitcast.171, bf16[1,4096,1024]{2,1,0:T(8,128)(2,1)} %param.15), kind=kOutput, calls=%fused_computation.18 | convolution fusion | flops 1074266112 | bytes 9699328 | tf_op jit(solution)/shard_map/dot_general | solution.py:34
  165.8 6.6 %convolution_convert_fusion = bf16[2,2048,1024]{2,1,0:T(8,128)(2,1)} fusion(bf16[2,128,1024]{2,1,0:T(8,128)(2,1)} %bitcast.160, bf16[128,2,2048]{0,2,1:T(8,128)(2,1)S(1)} %all-to-all-done.1), kind=kOutput, calls=%fused_computation.14 | convolution fusion | flops 1077936128 | bytes 9961472 | tf_op jit(solution)/shard_map/nsd,nse->nde/dot_general | solution.py:85
  172.4 2.0 convolution_convert_fusion.2
  174.4 2.1 convolution_convert_fusion.1
  176.5 10.0 %convert_reduce_fusion = f32[2048,1024]{1,0:T(8,128)} fusion(bf16[2,2048,1024]{2,1,0:T(8,128)(2,1)} %convolution_convert_fusion), kind=kLoop, calls=%fused_computation.3 | loop fusion | flops 6291456 | bytes 16777216 | tf_op jit(solution)/shard_map/reduce_sum | solution.py:92
  186.5 1.2 fusion.80
  187.8 1.2 fusion.79
  188.9 4.3 %collective-permute-start.1 = (bf16[32,4096]{1,0:T(8,128)(2,1)S(1)}, bf16[32,4096]{1,0:T(8,128)(2,1)S(1)}, u32[]{:S(2)}, u32[]{:S(2)}) collective-permute-start(bf16[32,4096]{1,0:T(8,128)(2,1)S(1)} %fusion.79), channel_id=1, source_target_pairs={{0,24},{8,0},{16,8},{24,16},{1,25},{9,1},{17,9},{25,17},{2,26},{10... | collective-permute-start | bytes 786440 | tf_op jit(solution)/shard_map/ppermute | solution.py:14
  193.2 2.5 %reduce-scatter.3.cloned.1.call-done = bf16[32,4096]{1,0:T(8,128)(2,1)} async-done(((bf16[128,4096]{1,0:T(8,128)(2,1)}), bf16[32,4096]{1,0:T(8,128)(2,1)}) %reduce-scatter.3.cloned.1.call-update) | async-done | bytes 262160 | tf_op jit(solution)/shard_map/reduce_scatter | solution.py:144
  195.7 1.0 fusion.84
  196.8 2.2 %collective-permute-start = (bf16[32,4096]{1,0:T(8,128)(2,1)S(1)}, bf16[32,4096]{1,0:T(8,128)(2,1)S(1)}, u32[]{:S(2)}, u32[]{:S(2)}) collective-permute-start(bf16[32,4096]{1,0:T(8,128)(2,1)S(1)} %fusion.84), channel_id=1, source_target_pairs={{0,8},{8,16},{16,24},{24,0},{1,9},{9,17},{17,25},{25,1},{2,10},{10... | collective-permute-start | bytes 786440 | tf_op jit(solution)/shard_map/ppermute | solution.py:14
  199.0 3.5 %convert_reduce_fusion.2 = f32[2048,256]{1,0:T(8,128)} fusion(bf16[2,2048,256]{2,1,0:T(8,128)(2,1)} %convolution_convert_fusion.2), kind=kLoop, calls=%fused_computation.20 | loop fusion | flops 1572864 | bytes 4194304 | tf_op jit(solution)/shard_map/reduce_sum | solution.py:92
  202.4 1.7 convert_reduce_fusion.1
  204.2 0.7 copy.87
  204.9 0.7 copy.88
  (42 shorter events, 0.2 us)
Async XLA Ops:
  7.2 59.4 %copy-start = (bf16[1,4096,256]{2,1,0:T(8,128)(2,1)S(1)}, bf16[1,4096,256]{2,1,0:T(8,128)(2,1)}, u32[]{:S(2)}) copy-start(bf16[1,4096,256]{2,1,0:T(8,128)(2,1)} %param.13) | copy-start | bytes 6291460
  7.2 62.7 %all-gather.6.cloned.1.call-start = ((), (), s32[]{:S(2)}) async-start(), calls=%async_computation.7 | async-start | bytes 1310720 | tf_op jit(solution)/shard_map/all_gather | solution.py:107
  7.9 9.3 %copy-start.4 = (bf16[1,1,32,4096]{3,2,1,0:T(8,128)(2,1)S(1)}, bf16[1,1,32,4096]{3,2,1,0:T(8,128)(2,1)}, u32[]{:S(2)}) copy-start(bf16[1,1,32,4096]{3,2,1,0:T(8,128)(2,1)} %param.8) | copy-start | bytes 786436
  9.1 0.6 copy-start.11
  10.7 7.5 %copy-start.13 = (s32[1,1,2,128]{3,2,1,0:T(2,128)S(1)}, s32[1,1,2,128]{3,2,1,0:T(2,128)}, u32[]{:S(2)}) copy-start(s32[1,1,2,128]{3,2,1,0:T(2,128)} %param.11) | copy-start | bytes 3076
  11.8 47.5 %all-to-all-start = ((bf16[4,32,4096]{2,1,0:T(8,128)(2,1)}), bf16[4,32,4096]{2,1,0:T(8,128)(2,1)S(1)}, u32[]{:S(2)}, u32[]{:S(2)}) async-start(bf16[4,32,4096]{2,1,0:T(8,128)(2,1)} %stack.2), calls=%async_computation.1 | async-start | bytes 2097152 | tf_op jit(solution)/shard_map/all_to_all | solution.py:105
  17.2 122.6 %all-gather.4.cloned.1.call-start = ((), (), s32[]{:S(2)}) async-start(), calls=%async_computation.4 | async-start | bytes 1310720 | tf_op jit(solution)/shard_map/all_gather | solution.py:103
  69.9 7.5 %copy-start.9 = (bf16[128,2,128,1]{0,2,3,1:T(8,128)(2,1)S(1)}, bf16[128,2,128,1]{0,2,3,1:T(8,128)(2,1)}, u32[]{:S(2)}) copy-start(bf16[128,2,128,1]{0,2,3,1:T(8,128)(2,1)} %copy.54) | copy-start | bytes 196612
  105.4 60.4 %all-to-all-start.1 = ((bf16[128,2,2048]{0,2,1:T(8,128)(2,1)}), bf16[128,2,2048]{0,2,1:T(8,128)(2,1)S(1)}, u32[]{:S(2)}, u32[]{:S(2)}) async-start(bf16[128,2,2048]{0,2,1:T(8,128)(2,1)} %copy.45), calls=%async_computation.3 | async-start | bytes 2097152 | tf_op jit(solution)/shard_map/all_to_all | solution.py:161
  109.0 77.6 %reduce-scatter.5.cloned.1.call-start = ((), (), s32[]{:S(2)}) async-start(), calls=%async_computation.6 | async-start | bytes 1310720 | tf_op jit(solution)/shard_map/reduce_scatter | solution.py:147
  129.7 6.4 %copy-start.8 = (bf16[2,128,128]{2,1,0:T(8,128)(2,1)S(1)}, bf16[2,128,128]{2,1,0:T(8,128)(2,1)}, u32[]{:S(2)}) copy-start(bf16[2,128,128]{2,1,0:T(8,128)(2,1)} %fusion.60) | copy-start | bytes 196612
  136.2 1.6 copy-start.1
  139.6 56.1 %reduce-scatter.3.cloned.1.call-start = ((), (), s32[]{:S(2)}) async-start(), calls=%async_computation.5 | async-start | bytes 1310720 | tf_op jit(solution)/shard_map/reduce_scatter | solution.py:144
  152.2 3.9 %copy-start.10 = (bf16[128,256]{0,1:T(8,128)(2,1)S(1)}, bf16[128,256]{0,1:T(8,128)(2,1)}, u32[]{:S(2)}) copy-start(bf16[128,256]{0,1:T(8,128)(2,1)} %copy.60) | copy-start | bytes 196612
  165.8 6.6 %copy-start.6 = (bf16[256,256]{1,0:T(8,128)(2,1)S(1)}, bf16[256,256]{1,0:T(8,128)(2,1)}, u32[]{:S(2)}) copy-start(bf16[256,256]{1,0:T(8,128)(2,1)} %copy.47) | copy-start | bytes 393220
  172.4 2.0 copy-start.7
  176.5 10.0 %copy-start.3 = (bf16[1,1,32,4096]{3,2,1,0:T(8,128)(2,1)S(1)}, bf16[1,1,32,4096]{3,2,1,0:T(8,128)(2,1)}, u32[]{:S(2)}) copy-start(bf16[1,1,32,4096]{3,2,1,0:T(8,128)(2,1)} %param.9) | copy-start | bytes 786436
  176.5 10.0 %copy-start.12 = (f32[32]{0:T(128)S(1)}, f32[32]{0:T(128)}, u32[]{:S(2)}) copy-start(f32[32]{0:T(128)} %copy-done.11) | copy-start | bytes 388
  176.5 11.3 %copy-start.5 = (bf16[1,1,32,4096]{3,2,1,0:T(8,128)(2,1)S(1)}, bf16[1,1,32,4096]{3,2,1,0:T(8,128)(2,1)}, u32[]{:S(2)}) copy-start(bf16[1,1,32,4096]{3,2,1,0:T(8,128)(2,1)} %param.10) | copy-start | bytes 786436
  188.9 15.2 %collective-permute-start.1 = (bf16[32,4096]{1,0:T(8,128)(2,1)S(1)}, bf16[32,4096]{1,0:T(8,128)(2,1)S(1)}, u32[]{:S(2)}, u32[]{:S(2)}) collective-permute-start(bf16[32,4096]{1,0:T(8,128)(2,1)S(1)} %fusion.79), channel_id=1, source_target_pairs={{0,24},{8,0},{16,8},{24,16},{1,25},{9,1},{17,9},{25,17},{2,26},{10... | collective-permute-start | bytes 786440 | tf_op jit(solution)/shard_map/ppermute | solution.py:14
  196.8 5.7 %copy-start.2 = (bf16[2,2048,256]{2,1,0:T(8,128)(2,1)S(1)}, bf16[2,2048,256]{2,1,0:T(8,128)(2,1)}, u32[]{:S(2)}) copy-start(bf16[2,2048,256]{2,1,0:T(8,128)(2,1)} %convolution_convert_fusion.1) | copy-start | bytes 6291460
  196.8 7.4 %collective-permute-start = (bf16[32,4096]{1,0:T(8,128)(2,1)S(1)}, bf16[32,4096]{1,0:T(8,128)(2,1)S(1)}, u32[]{:S(2)}, u32[]{:S(2)}) collective-permute-start(bf16[32,4096]{1,0:T(8,128)(2,1)S(1)} %fusion.84), channel_id=1, source_target_pairs={{0,8},{8,16},{16,24},{24,0},{1,9},{9,17},{17,25},{25,1},{2,10},{10... | collective-permute-start | bytes 786440 | tf_op jit(solution)/shard_map/ppermute | solution.py:14
Sparse Core Ops, SparseCore 0:
  9.6 49.1 all-gather.5
  60.9 27.1 all-gather.3
  139.7 27.4 reduce-scatter.4
  169.9 25.7 reduce-scatter.2
